TPU v7x, 32 devices: a whole 2x2x4 slice. The times are simulated.
32 devices in a mesh: rows: 8 (over z, y), cols: 4 (over x, core).
Axes of the slice: x: 2, y: 2, z: 4, core: 2. Of those that a mesh axis runs over, the one named last changes fastest.
Arguments:
- factor_a: bfloat16 [16384, 48, 48], P('rows'), may hold values from -0.875 to 0.875
- factor_b: bfloat16 [16384, 48, 48], P('rows'), may hold values from -0.046875 to 0.046875
- next_factor: bfloat16 [16384, 48, 48], P(('rows', 'cols')), may hold values from -6 to 6
- sketch_leg: bfloat16 [48, 32], replicated, may hold values from -6 to 6
- sketch_rows: bfloat16 [16384, 32], P('rows', 'cols'), may hold values from -6 to 6
Outputs:
- basis: float32 [32, 16384, 48], P(None, ('rows', 'cols'))
- squeezed: float32 [32, 48], replicated
All inputs are finite; a program needn't handle non-finite values.
Results may differ from a plain program's by a relative error of at most 0.0003.
Values sent between devices are 32-bit elements; how exact they have to be, the bound alone decides.
No kernel may reach another device: no remote copies, remote signals or barrier semaphores. Data moves between devices by JAX's collectives and lax.ppermute only.
A program may use at most 128 MiB of HBM per device.

v0:
```python
import jax
import jax.numpy as jnp
from jax import lax
from jax.sharding import PartitionSpec as P


def per_device(factor_a, factor_b, next_factor, sketch_leg, sketch_rows):
    high = lax.Precision.HIGHEST
    local_rows = factor_a.shape[0]
    width = factor_a.shape[1]
    col_parts = lax.axis_size("cols")
    quarter = local_rows // col_parts
    col_index = lax.axis_index("cols")
    count = local_rows * lax.axis_size("rows") * width
    start = col_index * quarter
    far_part = jnp.einsum("sp,syk->pyk", sketch_rows, factor_b, preferred_element_type=jnp.float32)
    far = lax.psum(far_part, "rows")
    far_all = lax.all_gather(far, "cols", axis=0, tiled=True)
    own_rows = lax.dynamic_slice_in_dim(factor_a, start, quarter, 0)
    near = jnp.einsum("sxk,xp->psk", own_rows, sketch_leg, preferred_element_type=jnp.float32)
    sketch = jnp.einsum("psk,pyk->psy", near, far_all, precision=high)
    columns = sketch.shape[0]
    flat = sketch.reshape(columns, quarter * width)
    own_next = next_factor.reshape(quarter * width, width).astype(jnp.float32)
    gram_part = jnp.dot(flat, flat.T, precision=high)
    root_count = jnp.sqrt(jnp.float32(count))
    gram = lax.psum(gram_part, ("rows", "cols")) / count
    lower = jnp.linalg.cholesky(gram)
    basis = jax.scipy.linalg.solve_triangular(lower, flat, lower=True)
    squeeze_part = jnp.dot(basis, own_next, precision=high)
    squeezed = lax.psum(squeeze_part, ("rows", "cols")) / root_count
    return (basis.reshape(columns, quarter, width), squeezed)


def solution(mesh):
    return jax.shard_map(
        per_device,
        mesh=mesh,
        in_specs=(
            P("rows", None, None),
            P("rows", None, None),
            P(("rows", "cols"), None, None),
            P(),
            P("rows", "cols"),
        ),
        out_specs=(P(None, ("rows", "cols"), None), P()),
        check_vma=False,
    )
```

profile of v0, /device:TPU:0, one launch (start us, length us, event | category | flops | bytes accessed | tf_op | source)
XLA Modules:
  0.0 238.8 jit_solution(5856863479625042245)
XLA Ops:
  7.2 0.7 copy-done
  7.9 8.9 %fusion.12 = f32[8,48,48]{2,0,1:T(8,128)} fusion(bf16[2048,48,48]{0,2,1:T(8,128)(2,1)} %param.6, bf16[2048,8]{0,1:T(8,128)(2,1)S(1)} %copy-done), kind=kOutput, calls=%fused_computation.8 | convolution fusion | flops 75497472 | bytes 9543680 | tf_op jit(solution)/shard_map/sp,syk->pyk/dot_general | solution.py:16
  16.9 1.8 constant_dynamic-slice_fusion
  18.7 3.4 %fusion.6 = f32[32,512,48]{1,0,2:T(8,128)} fusion(bf16[512,48,48]{0,2,1:T(8,128)(2,1)S(1)} %constant_dynamic-slice_fusion, bf16[48,32]{0,1:T(8,128)(2,1)S(1)} %copy-done.2), kind=kOutput, calls=%fused_computation.6 | convolution fusion | flops 75497472 | bytes 5508096 | tf_op jit(solution)/shard_map/sxk,xp->psk/dot_general | solution.py:20
  22.1 5.0 %copy.27 = bf16[512,48,48]{1,0,2:T(8,128)(2,1)} copy(bf16[512,48,48]{0,2,1:T(8,128)(2,1)S(1)} %copy-done.1) | data formatting | bytes 4718592 | tf_op args[2]
  27.2 14.0 %reshape.25 = bf16[24576,48]{0,1:T(8,128)(2,1)} reshape(bf16[512,48,48]{1,0,2:T(8,128)(2,1)} %copy.27) | data formatting | bytes 4718592 | tf_op jit(solution)/shard_map/reshape | solution.py:24
  41.1 49.3 %all-reduce.2.cloned.1.call-done = f32[8,48,48]{2,0,1:T(8,128)} async-done(((f32[8,48,48]{2,0,1:T(8,128)}), f32[8,48,48]{2,0,1:T(8,128)}) %all-reduce.2.cloned.1.call-update) | async-done | bytes 73744 | tf_op jit(solution)/shard_map/psum | solution.py:17
  90.4 1.0 copy.20
  91.4 8.8 %all_gather.3 = f32[32,48,48]{2,1,0:T(8,128)S(1)} all-gather(f32[8,48,48]{2,1,0:T(8,128)S(1)} %copy.20), channel_id=1, replica_groups=mesh['rows'=8,'cols'=4] {'cols'}, dimensions={0}, use_global_device_ids=true | all-gather | bytes 368640 | tf_op jit(solution)/shard_map/all_gather | solution.py:18
  100.1 6.7 %fusion.2 = f32[32,512,48]{1,2,0:T(8,128)S(1)} fusion(f32[32,48,48]{2,1,0:T(8,128)S(1)} %all_gather.3, f32[32,512,48]{1,0,2:T(8,128)} %fusion.6), kind=kOutput, calls=%fused_computation.2 | convolution fusion | flops 452984832 | bytes 6586368 | tf_op jit(solution)/shard_map/psk,pyk->psy/dot_general | solution.py:21
  106.9 4.2 %fusion.9 = f32[32,32]{0,1:T(8,128)S(1)} fusion(f32[32,512,48]{1,2,0:T(8,128)S(1)} %fusion.2), kind=kOutput, calls=%fused_computation.7 | convolution fusion | flops 301989888 | bytes 3149824 | tf_op jit(solution)/shard_map/dot_general | solution.py:25
  111.1 4.7 %copy.26 = f32[32,512,48]{2,1,0:T(8,128)} copy(f32[32,512,48]{1,2,0:T(8,128)S(1)} %fusion.2) | data formatting | bytes 6291456 | tf_op jit(solution)/shard_map/psk,pyk->psy/dot_general | solution.py:21
  115.8 38.7 %psum.22 = f32[32,32]{0,1:T(8,128)S(1)} all-reduce(f32[32,32]{0,1:T(8,128)S(1)} %fusion.9), channel_id=1, replica_groups=mesh['rows'=8,'cols'=4] {'rows','cols'}, use_global_device_ids=true, to_apply=%region_1.0 | all-reduce | flops 1024 | bytes 8192 | tf_op jit(solution)/shard_map/psum | solution.py:27
  154.5 2.9 %cholesky.16 = f32[32,32]{1,0:T(8,128)S(1)} custom-call(f32[32,32]{1,0:T(8,128)S(1)} %fusion.17), custom_call_target="Cholesky" | custom-call | tf_op jit(solution)/shard_map/jit(cholesky)/cholesky | solution.py:28
  157.5 0.6 compare_reduce_fusion
  158.1 0.7 fusion.14
  158.8 2.4 %custom-call.7 = f32[1,32,32]{1,2,0:T(8,128)S(1)} custom-call(f32[1,32,32]{2,1,0:T(8,128)S(1)} %fusion.14), custom_call_target="InvertDiagBlocksLowerTriangular" | custom-call | tf_op jit(solution)/shard_map/jit(_solve_triangular)/triangular_solve | solution.py:29
  161.2 9.8 %reshape.23 = f32[32,24576]{1,0:T(8,128)} reshape(f32[32,512,48]{2,1,0:T(8,128)} %copy.26) | data formatting | bytes 6291456 | tf_op jit(solution)/shard_map/reshape | solution.py:23
  171.0 4.6 %fusion.15 = f32[32,24576]{1,0:T(8,128)S(1)} fusion(f32[32,24576]{1,0:T(8,128)} %reshape.23, f32[1,32,32]{1,2,0:T(8,128)S(1)} %custom-call.7), kind=kOutput, calls=%fused_computation.12 | convolution fusion | flops 301989888 | bytes 6295552 | tf_op jit(solution)/shard_map/jit(_solve_triangular)/triangular_solve | solution.py:29
  175.6 5.4 %reshape.24 = f32[32,512,48]{2,1,0:T(8,128)} reshape(f32[32,24576]{1,0:T(8,128)S(1)} %fusion.15) | data formatting | bytes 6291456 | tf_op jit(solution)/shard_map/reshape | solution.py:32
  181.0 3.7 %fusion.19 = f32[32,48]{1,0:T(8,128)S(1)} fusion(f32[32,24576]{1,0:T(8,128)S(1)} %fusion.15, bf16[24576,48]{0,1:T(8,128)(2,1)} %reshape.25), kind=kOutput, calls=%fused_computation.24 | convolution fusion | flops 452984832 | bytes 5511168 | tf_op jit(solution)/shard_map/dot_general | solution.py:30
  184.7 40.1 %psum.23 = f32[32,48]{1,0:T(8,128)S(1)} all-reduce(f32[32,48]{1,0:T(8,128)S(1)} %fusion.19), channel_id=1, replica_groups=mesh['rows'=8,'cols'=4] {'rows','cols'}, use_global_device_ids=true, to_apply=%region_4.5 | all-reduce | flops 1536 | bytes 12288 | tf_op jit(solution)/shard_map/psum | solution.py:31
  224.8 0.6 broadcast_multiply_fusion
  225.5 6.5 %copy.28 = f32[32,512,48]{1,2,0:T(8,128)} copy(f32[32,512,48]{2,1,0:T(8,128)} %reshape.24) | data formatting | bytes 6291456
  (11 shorter events, 0.2 us)
Async XLA Ops:
  7.2 0.8 copy-start
  7.2 83.2 %all-reduce.2.cloned.1.call-start = ((), (), s32[]{:S(2)}) async-start(), calls=%async_computation | async-start | bytes 393216 | tf_op jit(solution)/shard_map/psum | solution.py:17
  16.8 1.9 copy-start.2
  18.7 3.4 %copy-start.1 = (bf16[512,48,48]{0,2,1:T(8,128)(2,1)S(1)}, bf16[512,48,48]{0,2,1:T(8,128)(2,1)}, u32[]{:S(2)}) copy-start(bf16[512,48,48]{0,2,1:T(8,128)(2,1)} %param.7) | copy-start | bytes 7077892
Sparse Core Ops, SparseCore 0:
  17.0 73.3 all-reduce.1
where the time goes:
time: 239 us
  blocking collectives  87.6 us (37%)
  waiting for transfers between devices  49.3 us (21%)
  local copies, waits for them, and re-layouts  48.9 us (20%)
  matrix products  31.5 us (13%)
  between operations  14.1 us (6%)
  other arithmetic  7.3 us (3%)
    psum x1, waiting for transfers between devices, per_device(): far = lax.psum(far_part, 'rows')  49.3 us
    psum x1, blocking collectives, per_device(): squeezed = lax.psum(squeeze_part, ('rows', 'cols')) / root_count  40.1 us
    psum x1, blocking collectives, per_device(): gram = lax.psum(gram_part, ('rows', 'cols')) / count  38.7 us
    reshape x1, local copies, waits for them, and re-layouts, per_device(): own_next = next_factor.reshape(quarter * width, width).astype(jnp.float32)  14 us
    unnamed x8, local copies, waits for them, and re-layouts  12.3 us
    reshape x1, local copies, waits for them, and re-layouts, per_device(): flat = sketch.reshape(columns, quarter * width)  9.77 us
    dot_general x1, matrix products, per_device(): jnp.einsum('sp,syk->pyk', sketch_rows, factor_b, preferred_element_type=j...  8.91 us
    all_gather x1, blocking collectives, per_device(): far_all = lax.all_gather(far, 'cols', axis=0, tiled=True)  8.76 us
  transfers between devices with their start and end apart: 1, of which 1 were waited for; matrix products, arithmetic and copies ran while one was open for 10% of the time, Pallas kernels for 0%

commit v1 on v0

--- a/solution.py
+++ b/solution.py
@@ -14,7 +14,9 @@
     count = local_rows * lax.axis_size("rows") * width
     start = col_index * quarter
     far_part = jnp.einsum("sp,syk->pyk", sketch_rows, factor_b, preferred_element_type=jnp.float32)
-    far = lax.psum(far_part, "rows")
+    far = far_part
+    for hop in (1, 2, 4):
+        far = far + lax.ppermute(far, "rows", [(dev, dev ^ hop) for dev in range(8)])
     far_all = lax.all_gather(far, "cols", axis=0, tiled=True)
     own_rows = lax.dynamic_slice_in_dim(factor_a, start, quarter, 0)
     near = jnp.einsum("sxk,xp->psk", own_rows, sketch_leg, preferred_element_type=jnp.float32)

time: 239 us -> 190 us (0.79)
  waiting for transfers between devices: 49.3 us -> 7.33 us
  between operations: 14.1 us -> 0.72 us
  starting transfers between devices: 0.04 us -> 7.47 us
    psum x1 -> x0, waiting for transfers between devices: 49.3 us -> none  [per_device(): far = lax.psum(far_part, 'rows')]
    ppermute x0 -> x3, starting transfers between devices: none -> 7.47 us  [per_device(): lax.ppermute(far, 'rows', [(dev, dev ^ hop) for dev in range(8)])]
    ppermute x0 -> x3, waiting for transfers between devices: none -> 7.33 us  [per_device(): lax.ppermute(far, 'rows', [(dev, dev ^ hop) for dev in range(8)])]
    unnamed x8 -> x10, local copies, waits for them, and re-layouts: 12.3 us -> 12.3 us
  transfers between devices with their start and end apart: 1 -> 3, of which waited for: 1 -> 2; matrix products, arithmetic and copies ran while one was open for 10% -> 13% of each run, Pallas kernels for 0% -> 0%
where the time goes in v1:
time: 190 us; the launch traced here: 189 us
  blocking collectives  88.3 us (46%)
  local copies, waits for them, and re-layouts  48 us (25%)
  matrix products  29.7 us (16%)
  starting transfers between devices  7.47 us (4%)
  other arithmetic  7.36 us (4%)
  waiting for transfers between devices  7.33 us (4%)
    psum x1, blocking collectives, per_device(): squeezed = lax.psum(squeeze_part, ('rows', 'cols')) / root_count  40 us
    psum x1, blocking collectives, per_device(): gram = lax.psum(gram_part, ('rows', 'cols')) / count  39.5 us
    reshape x1, local copies, waits for them, and re-layouts, per_device(): own_next = next_factor.reshape(quarter * width, width).astype(jnp.float32)  14 us
    unnamed x10, local copies, waits for them, and re-layouts  12.3 us
    reshape x1, local copies, waits for them, and re-layouts, per_device(): flat = sketch.reshape(columns, quarter * width)  9.77 us
    all_gather x1, blocking collectives, per_device(): far_all = lax.all_gather(far, 'cols', axis=0, tiled=True)  8.78 us
    ppermute x3, starting transfers between devices, per_device(): lax.ppermute(far, 'rows', [(dev, dev ^ hop) for dev in range(8)])  7.47 us
    ppermute x3, waiting for transfers between devices, per_device(): lax.ppermute(far, 'rows', [(dev, dev ^ hop) for dev in range(8)])  7.33 us
  transfers between devices with their start and end apart: 3, of which 2 were waited for; matrix products, arithmetic and copies ran while one was open for 13% of the time, Pallas kernels for 0%

profile of v1, /device:TPU:0, one launch (start us, length us, event | category | flops | bytes accessed | tf_op | source)
XLA Modules:
  0.0 188.9 jit_solution(4254687292305546478)
XLA Ops:
  0.6 0.7 copy-done
  1.4 7.0 %fusion.11 = f32[8,48,48]{2,0,1:T(8,128)S(1)} fusion(bf16[2048,48,48]{0,2,1:T(8,128)(2,1)} %param.6, bf16[2048,8]{0,1:T(8,128)(2,1)S(1)} %copy-done), kind=kOutput, calls=%fused_computation.9 | convolution fusion | flops 75497472 | bytes 9543680 | tf_op jit(solution)/shard_map/sp,syk->pyk/dot_general | solution.py:16
  8.4 3.0 %collective-permute-start = (f32[8,48,48]{2,0,1:T(8,128)S(1)}, f32[8,48,48]{2,0,1:T(8,128)S(1)}, u32[]{:S(2)}, u32[]{:S(2)}) collective-permute-start(f32[8,48,48]{2,0,1:T(8,128)S(1)} %fusion.11), channel_id=1, source_target_pairs={{0,4},{4,0},{8,12},{12,8},{16,20},{20,16},{24,28},{28,24},{1,5},{5... | collective-permute-start | bytes 221192 | tf_op jit(solution)/shard_map/ppermute | solution.py:19
  11.4 4.9 %collective-permute-done = f32[8,48,48]{2,0,1:T(8,128)S(1)} collective-permute-done((f32[8,48,48]{2,0,1:T(8,128)S(1)}, f32[8,48,48]{2,0,1:T(8,128)S(1)}, u32[]{:S(2)}, u32[]{:S(2)}) %collective-permute-start) | collective-permute-done | bytes 73760 | tf_op jit(solution)/shard_map/ppermute | solution.py:19
  16.3 1.9 collective-permute-start.1
  18.2 1.8 constant_dynamic-slice_fusion
  20.0 2.4 %collective-permute-done.1 = f32[8,48,48]{2,0,1:T(8,128)S(1)} collective-permute-done((f32[8,48,48]{2,0,1:T(8,128)S(1)}, f32[8,48,48]{2,0,1:T(8,128)S(1)}, u32[]{:S(2)}, u32[]{:S(2)}) %collective-permute-start.1) | collective-permute-done | bytes 73760 | tf_op jit(solution)/shard_map/ppermute | solution.py:19
  22.5 2.6 %collective-permute-start.2 = (f32[8,48,48]{2,0,1:T(8,128)S(1)}, f32[8,48,48]{2,0,1:T(8,128)S(1)}, u32[]{:S(2)}, u32[]{:S(2)}) collective-permute-start(f32[8,48,48]{2,0,1:T(8,128)S(1)} %add.30), channel_id=1, source_target_pairs={{0,16},{4,20},{8,24},{12,28},{16,0},{20,4},{24,8},{28,12},{1,17},{... | collective-permute-start | bytes 221192 | tf_op jit(solution)/shard_map/ppermute | solution.py:19
  25.1 3.4 %fusion.5 = f32[512,48,32]{0,2,1:T(8,128)} fusion(bf16[512,48,48]{0,2,1:T(8,128)(2,1)S(1)} %constant_dynamic-slice_fusion, bf16[48,32]{0,1:T(8,128)(2,1)S(1)} %copy-done.3), kind=kOutput, calls=%fused_computation.5 | convolution fusion | flops 75497472 | bytes 5508096 | tf_op jit(solution)/shard_map/sxk,xp->psk/dot_general | solution.py:22
  28.5 5.0 %copy.19 = bf16[512,48,48]{1,0,2:T(8,128)(2,1)} copy(bf16[512,48,48]{0,2,1:T(8,128)(2,1)S(1)} %copy-done.2) | data formatting | bytes 4718592 | tf_op args[2]
  33.5 14.0 %reshape.25 = bf16[24576,48]{0,1:T(8,128)(2,1)} reshape(bf16[512,48,48]{1,0,2:T(8,128)(2,1)} %copy.19) | data formatting | bytes 4718592 | tf_op jit(solution)/shard_map/reshape | solution.py:26
  47.5 8.8 %all_gather.3 = f32[32,48,48]{2,0,1:T(8,128)S(1)} all-gather(f32[8,48,48]{2,0,1:T(8,128)S(1)} %add.31), channel_id=1, replica_groups=mesh['rows'=8,'cols'=4] {'cols'}, dimensions={0}, use_global_device_ids=true | all-gather | bytes 368640 | tf_op jit(solution)/shard_map/all_gather | solution.py:20
  56.3 6.8 %fusion = f32[32,512,48]{1,2,0:T(8,128)S(1)} fusion(f32[512,48,32]{0,2,1:T(8,128)} %fusion.5, f32[32,48,48]{2,0,1:T(8,128)S(1)} %all_gather.3), kind=kOutput, calls=%fused_computation | convolution fusion | flops 452984832 | bytes 6586368 | tf_op jit(solution)/shard_map/psk,pyk->psy/dot_general | solution.py:23
  63.1 4.2 %fusion.7 = f32[32,32]{0,1:T(8,128)S(1)} fusion(f32[32,512,48]{1,2,0:T(8,128)S(1)} %fusion), kind=kOutput, calls=%fused_computation.7 | convolution fusion | flops 301989888 | bytes 3149824 | tf_op jit(solution)/shard_map/dot_general | solution.py:27
  67.3 4.7 %copy.18 = f32[32,512,48]{2,1,0:T(8,128)} copy(f32[32,512,48]{1,2,0:T(8,128)S(1)} %fusion) | data formatting | bytes 6291456 | tf_op jit(solution)/shard_map/psk,pyk->psy/dot_general | solution.py:23
  72.0 39.5 %psum.14 = f32[32,32]{0,1:T(8,128)S(1)} all-reduce(f32[32,32]{0,1:T(8,128)S(1)} %fusion.7), channel_id=1, replica_groups=mesh['rows'=8,'cols'=4] {'rows','cols'}, use_global_device_ids=true, to_apply=%region_0.0 | all-reduce | flops 1024 | bytes 8192 | tf_op jit(solution)/shard_map/psum | solution.py:29
  111.6 2.9 %cholesky.16 = f32[32,32]{1,0:T(8,128)S(1)} custom-call(f32[32,32]{1,0:T(8,128)S(1)} %fusion.16), custom_call_target="Cholesky" | custom-call | tf_op jit(solution)/shard_map/jit(cholesky)/cholesky | solution.py:30
  115.9 2.4 %custom-call.7 = f32[1,32,32]{1,2,0:T(8,128)S(1)} custom-call(f32[1,32,32]{2,1,0:T(8,128)S(1)} %fusion.13), custom_call_target="InvertDiagBlocksLowerTriangular" | custom-call | tf_op jit(solution)/shard_map/jit(_solve_triangular)/triangular_solve | solution.py:31
  118.3 9.8 %reshape.23 = f32[32,24576]{1,0:T(8,128)} reshape(f32[32,512,48]{2,1,0:T(8,128)} %copy.18) | data formatting | bytes 6291456 | tf_op jit(solution)/shard_map/reshape | solution.py:25
  128.1 4.6 %fusion.14 = f32[32,24576]{1,0:T(8,128)S(1)} fusion(f32[32,24576]{1,0:T(8,128)} %reshape.23, f32[1,32,32]{1,2,0:T(8,128)S(1)} %custom-call.7), kind=kOutput, calls=%fused_computation.13 | convolution fusion | flops 301989888 | bytes 6295552 | tf_op jit(solution)/shard_map/jit(_solve_triangular)/triangular_solve | solution.py:31
  132.7 5.4 %reshape.24 = f32[32,512,48]{2,1,0:T(8,128)} reshape(f32[32,24576]{1,0:T(8,128)S(1)} %fusion.14) | data formatting | bytes 6291456 | tf_op jit(solution)/shard_map/reshape | solution.py:34
  138.1 3.7 %fusion.18 = f32[32,48]{1,0:T(8,128)S(1)} fusion(f32[32,24576]{1,0:T(8,128)S(1)} %fusion.14, bf16[24576,48]{0,1:T(8,128)(2,1)} %reshape.25), kind=kOutput, calls=%fused_computation.25 | convolution fusion | flops 452984832 | bytes 5511168 | tf_op jit(solution)/shard_map/dot_general | solution.py:32
  141.8 40.0 %psum.15 = f32[32,48]{1,0:T(8,128)S(1)} all-reduce(f32[32,48]{1,0:T(8,128)S(1)} %fusion.18), channel_id=1, replica_groups=mesh['rows'=8,'cols'=4] {'rows','cols'}, use_global_device_ids=true, to_apply=%region_3.4 | all-reduce | flops 1536 | bytes 12288 | tf_op jit(solution)/shard_map/psum | solution.py:33
  182.4 6.5 %copy.20 = f32[32,512,48]{1,2,0:T(8,128)} copy(f32[32,512,48]{2,1,0:T(8,128)} %reshape.24) | data formatting | bytes 6291456
  (18 shorter events, 2.1 us)
Async XLA Ops:
  0.6 0.8 copy-start
  8.4 16.7 %copy-start.3 = (bf16[48,32]{0,1:T(8,128)(2,1)S(1)}, bf16[48,32]{0,1:T(8,128)(2,1)}, u32[]{:S(2)}) copy-start(bf16[48,32]{0,1:T(8,128)(2,1)} %param.8) | copy-start | bytes 9220
  8.4 7.9 %collective-permute-start = (f32[8,48,48]{2,0,1:T(8,128)S(1)}, f32[8,48,48]{2,0,1:T(8,128)S(1)}, u32[]{:S(2)}, u32[]{:S(2)}) collective-permute-start(f32[8,48,48]{2,0,1:T(8,128)S(1)} %fusion.11), channel_id=1, source_target_pairs={{0,4},{4,0},{8,12},{12,8},{16,20},{20,16},{24,28},{28,24},{1,5},{5... | collective-permute-start | bytes 221192 | tf_op jit(solution)/shard_map/ppermute | solution.py:19
  16.3 6.1 %collective-permute-start.1 = (f32[8,48,48]{2,0,1:T(8,128)S(1)}, f32[8,48,48]{2,0,1:T(8,128)S(1)}, u32[]{:S(2)}, u32[]{:S(2)}) collective-permute-start(f32[8,48,48]{2,0,1:T(8,128)S(1)} %add.29), channel_id=1, source_target_pairs={{0,8},{4,12},{8,0},{12,4},{16,24},{20,28},{24,16},{28,20},{1,9},{5... | collective-permute-start | bytes 221192 | tf_op jit(solution)/shard_map/ppermute | solution.py:19
  20.0 8.5 %copy-start.2 = (bf16[512,48,48]{0,2,1:T(8,128)(2,1)S(1)}, bf16[512,48,48]{0,2,1:T(8,128)(2,1)}, u32[]{:S(2)}) copy-start(bf16[512,48,48]{0,2,1:T(8,128)(2,1)} %param.7) | copy-start | bytes 7077892
  22.5 25.0 %collective-permute-start.2 = (f32[8,48,48]{2,0,1:T(8,128)S(1)}, f32[8,48,48]{2,0,1:T(8,128)S(1)}, u32[]{:S(2)}, u32[]{:S(2)}) collective-permute-start(f32[8,48,48]{2,0,1:T(8,128)S(1)} %add.30), channel_id=1, source_target_pairs={{0,16},{4,20},{8,24},{12,28},{16,0},{20,4},{24,8},{28,12},{1,17},{... | collective-permute-start | bytes 221192 | tf_op jit(solution)/shard_map/ppermute | solution.py:19
  181.8 7.1 %copy-start.1 = (bf16[2048,8]{0,1:T(8,128)(2,1)S(1)}, bf16[2048,8]{0,1:T(8,128)(2,1)}, u32[]{:S(2)}) copy-start(bf16[2048,8]{0,1:T(8,128)(2,1)} %param.9) | copy-start | bytes 98308
